TPU v7x, 64 devices: a 2x2x8 block of a 4x4x8 slice. The times are simulated.
64 devices in a mesh: rep: 4 (over x, y), dp: 16 (over z, core).
Axes of the slice: x: 2, y: 2, z: 8, core: 2. Of those that a mesh axis runs over, the one named last changes fastest.
The devices are a block of a 4x4x8 slice.
Arguments:
- x: bfloat16 [64, 4096, 512], P(('rep', 'dp')), parts along dimension 0
- dy: bfloat16 [64, 4096, 512], P(('rep', 'dp')), parts along dimension 0
- w_gate: bfloat16 [2, 512, 1408], P(None, 'dp')
- w_up: bfloat16 [2, 512, 1408], P(None, 'dp')
- w_down: bfloat16 [2, 1408, 512], P(None, 'dp')
Outputs:
- output 1: bfloat16 [64, 4096, 512], P(('rep', 'dp')), parts along dimension 0
- output 2: bfloat16 [8, 512, 1408], P('rep', 'dp'), parts along dimension 0
- output 3: bfloat16 [8, 512, 1408], P('rep', 'dp'), parts along dimension 0
- output 4: bfloat16 [8, 1408, 512], P('rep', 'dp'), parts along dimension 0
There are 4 independent parts. A program takes and returns all parts, laid end to end along the dimension named above; an argument that names none is the same for every part.
All inputs are finite; a program needn't handle non-finite values.
Results may differ from a plain program's by a relative error of at most 0.018.
Values are sent between devices in bfloat16 or wider.
A program may use at most 768 MiB of HBM per device.

v0:
```python
import jax
import jax.numpy as jnp
from jax import lax

NAMES = ("w_gate", "w_up", "w_down")


def matmul(a, w):
    return jnp.dot(a, w, preferred_element_type=jnp.float32).astype(jnp.bfloat16)


def normed(h):
    wide = h.astype(jnp.float32)
    scale = lax.rsqrt(jnp.mean(wide**2, -1, keepdims=True) + 1e-6)
    return (wide * scale).astype(jnp.bfloat16)


def layer(h, w):
    a = normed(h)
    gate = jnp.dot(a, w["w_gate"], preferred_element_type=jnp.float32)
    up = jnp.dot(a, w["w_up"], preferred_element_type=jnp.float32)
    return h + matmul((jax.nn.silu(gate) * up).astype(jnp.bfloat16), w["w_down"])


def stack(weights, h):
    for number in range(weights["w_gate"].shape[0]):
        h = layer(h, {name: w[number] for name, w in weights.items()})
    return h


def solution(mesh):
    groups = mesh.shape["rep"]

    def step(x, dy, *weights):
        shape = x.shape
        x, dy = (t.reshape(groups, -1, *t.shape[1:]) for t in (x, dy))

        def of_a_group(x, dy):
            _, back = jax.vjp(stack, dict(zip(NAMES, weights, strict=True)), x)
            by_weights, by_x = back(dy)
            return (by_x, *(by_weights[name] for name in NAMES))

        by_x, *by_weights = jax.vmap(of_a_group)(x, dy)
        return (by_x.reshape(shape), *(t.reshape(-1, *t.shape[2:]) for t in by_weights))

    return step
```

profile of v0, /device:TPU:22, one launch (start us, length us, event | category | flops | bytes accessed | tf_op | source)
XLA Modules:
  0.0 903.6 jit_solution(5722182161622689990)
XLA Ops:
  17.4 6.3 copy.1
  23.9 6.4 copy
  30.3 6.5 copy.3
  37.4 11.7 %all-gather.37.cloned.1.call-done = bf16[1,1408,512]{2,1,0:T(8,128)(2,1)} async-done(((bf16[1,88,512]{2,1,0:T(8,128)(2,1)}), bf16[1,1408,512]{2,1,0:T(8,128)(2,1)}) %all-gather.37.cloned.1.call-update) | async-done | bytes 1441808 | tf_op jit(solution)/vmap(jvp())/squeeze | solution.py:27
  49.1 11.4 %fusion.172 = bf16[1,1,4096,1408]{3,2,1,0:T(8,128)(2,1)} fusion(bf16[1,4096,512]{2,1,0:T(8,128)(2,1)} %param.12, bf16[1,1408,512]{2,1,0:T(8,128)(2,1)} %all-gather.37.cloned.1.call-done), kind=kOutput, calls=%fused_computation.208 | convolution fusion | flops 5911347200 | bytes 17170432 | tf_op jit(solution)/vmap(transpose(jvp()))/dot_general | solution.py:9
  60.5 24.4 %all-gather.29.cloned.1.call-done = bf16[1,512,1408]{2,1,0:T(8,128)(2,1)} async-done(((bf16[1,32,1408]{2,1,0:T(8,128)(2,1)}), bf16[1,512,1408]{2,1,0:T(8,128)(2,1)}) %all-gather.29.cloned.1.call-update) | async-done | bytes 1441808 | tf_op jit(solution)/vmap(jvp())/squeeze | solution.py:27
  84.8 13.1 %fusion.232 = f32[4096,1408]{1,0:T(8,128)} fusion(bf16[1,4096,512]{2,1,0:T(8,128)(2,1)} %param.13, f32[4096]{0:T(1024)S(1)} %get-tuple-element.267, bf16[1,512,1408]{2,1,0:T(8,128)(2,1)} %all-gather.29.cloned.1.call-done), kind=kOutput, calls=%fused_computation.252 | convolution fusion | flops 5911871488 | bytes 28721152 | tf_op jit(solution)/vmap(jvp())/dot_general | solution.py:20
  98.0 22.6 %all-gather.31.cloned.1.call-done = bf16[1,512,1408]{2,1,0:T(8,128)(2,1)} async-done(((bf16[1,32,1408]{2,1,0:T(8,128)(2,1)}), bf16[1,512,1408]{2,1,0:T(8,128)(2,1)}) %all-gather.31.cloned.1.call-update) | async-done | bytes 1441808 | tf_op jit(solution)/vmap(jvp())/squeeze | solution.py:27
  120.6 24.2 %fusion.168 = (bf16[1,1,4096,1408]{3,2,1,0:T(8,128)(2,1)}, f32[4096,1408]{1,0:T(8,128)}) fusion(f32[4096,1408]{1,0:T(8,128)} %fusion.232, bf16[1,512,1408]{2,1,0:T(8,128)(2,1)} %all-gather.31.cloned.1.call-done, bf16[1,4096,512]{2,1,0:T(8,128)(2,1)} %param.13, f32[4096]{0:T(1024)S(1)} %get-tuple-element.267), kind=kOutput, calls=%fused_computation.195 | convolution fusion | flops 5946474496 | bytes 63324160 | tf_op jit(solution)/vmap(jvp())/dot_general | solution.py:21
  144.8 11.5 %all-gather.33.cloned.1.call-done = bf16[1,1408,512]{2,1,0:T(8,128)(2,1)} async-done(((bf16[1,88,512]{2,1,0:T(8,128)(2,1)}), bf16[1,1408,512]{2,1,0:T(8,128)(2,1)}) %all-gather.33.cloned.1.call-update) | async-done | bytes 1441808 | tf_op jit(solution)/vmap(jvp())/squeeze | solution.py:27
  156.3 12.7 %fusion.184 = (f32[4096]{0:T(1024)S(1)}, bf16[1,1,4096,512]{2,3,1,0:T(8,128)(2,1)}) fusion(bf16[1,1408,512]{2,1,0:T(8,128)(2,1)} %all-gather.33.cloned.1.call-done, bf16[1,1,4096,1408]{3,2,1,0:T(8,128)(2,1)} %get-tuple-element.268, bf16[1,4096,512]{1,2,0:T(8,128)(2,1)} %copy.1), kind=kOutput, calls=%fused_computation.227 | convolution fusion | flops 5916061696 | bytes 21381120 | tf_op jit(solution)/vmap(jvp())/dot_general | solution.py:9
  169.0 15.0 %copy.4 = bf16[1,1,4096,1408]{2,3,1,0:T(8,128)(2,1)} copy(bf16[1,1,4096,1408]{3,2,1,0:T(8,128)(2,1)} %get-tuple-element.268) | data formatting | bytes 23068672
  184.6 5.3 fusion.185
  191.9 13.1 %fusion.226 = f32[4096,1408]{1,0:T(8,128)} fusion(bf16[1,1,4096,512]{2,3,1,0:T(8,128)(2,1)} %fusion.185, bf16[1,512,1408]{2,1,0:T(8,128)(2,1)} %all-gather.39.cloned.1.call-done), kind=kOutput, calls=%fused_computation.247 | convolution fusion | flops 5905580032 | bytes 28704768 | tf_op jit(solution)/vmap(jvp())/dot_general | solution.py:21
  205.0 22.5 %all-gather.35.cloned.1.call-done = bf16[1,512,1408]{2,1,0:T(8,128)(2,1)} async-done(((bf16[1,32,1408]{2,1,0:T(8,128)(2,1)}), bf16[1,512,1408]{2,1,0:T(8,128)(2,1)}) %all-gather.35.cloned.1.call-update) | async-done | bytes 1441808 | tf_op jit(solution)/vmap(jvp())/squeeze | solution.py:27
  227.5 35.2 %fusion.153 = (bf16[1,1,4096,1408]{3,2,1,0:T(8,128)(2,1)}, bf16[1,1,4096,1408]{3,2,1,0:T(8,128)(2,1)}, f32[4096,1408]{1,0:T(8,128)}) fusion(f32[4096,1408]{1,0:T(8,128)} %fusion.226, bf16[1,1,4096,1408]{3,2,1,0:T(8,128)(2,1)} %fusion.172, bf16[1,512,1408]{2,1,0:T(8,128)(2,1)} %all-gather.35.cloned.1.call-done, bf16[1,1,4096,512]{2,3,1,0:T(8,128)(2,1)} %fusion.185), kind=kOutput, calls=%fused_computation.175 | convolution fusion | flops 5992087552 | bytes 86376448 | tf_op jit(solution)/vmap(jvp())/dot_general | solution.py:20
  262.7 19.6 %fusion.162 = bf16[1,1,4096,1408]{3,2,1,0:T(8,128)(2,1)} fusion(f32[4096,1408]{1,0:T(8,128)} %fusion.226, f32[4096,1408]{1,0:T(8,128)} %get-tuple-element.272), kind=kLoop, calls=%fused_computation.185 | loop fusion | flops 34603008 | bytes 57671680 | tf_op jit(solution)/vmap(jvp())/convert_element_type | solution.py:22
  282.3 15.1 %copy.2 = bf16[1,1,4096,1408]{2,3,1,0:T(8,128)(2,1)} copy(bf16[1,1,4096,1408]{3,2,1,0:T(8,128)(2,1)} %fusion.162) | data formatting | bytes 23068672
  297.5 68.7 %while.16 = (bf16[1,1,4096,1408]{2,3,1,0:T(8,128)(2,1)}, bf16[1,1,4096,512]{3,2,1,0:T(8,128)(2,1)}, f32[1,88,512]{2,1,0:T(8,128)S(1)}, f32[1,88,512]{2,1,0:T(8,1...) while((bf16[1,1,4096,1408]{2,3,1,0:T(8,128)(2,1)}, ...), condition=%wide.windowed_dot_general_cond_rs.4.clone, body=%wide.windowed_dot_general_body_rs.4.clone.sunk | while | flops 1482432512 | bytes 37945956 | solution.py:9
  366.2 9.7 %fusion.190 = bf16[4096,512]{0,1:T(8,128)(2,1)S(1)} fusion(bf16[1,1,4096,1408]{3,2,1,0:T(8,128)(2,1)} %get-tuple-element.628, bf16[1,512,1408]{2,1,0:T(8,128)(2,1)S(1)} %copy-done.30), kind=kOutput, calls=%fused_computation.231 | convolution fusion | flops 5905580032 | bytes 17170432 | tf_op jit(solution)/vmap(transpose(jvp()))/dot_general | solution.py:21
  375.9 10.3 %fusion.186 = (f32[4096]{0:T(1024)S(1)}, bf16[1,1,4096,512]{2,3,1,0:T(8,128)(2,1)S(1)}) fusion(bf16[1,1,4096,512]{2,3,1,0:T(8,128)(2,1)S(1)} %copy-done.3, bf16[4096,512]{0,1:T(8,128)(2,1)S(1)} %fusion.190, bf16[1,512,1408]{2,1,0:T(8,128)(2,1)S(1)} %copy-done.31, bf16[1,1,4096,1408]{3,2,1,0:T(8,128)(2,1)} %get-tuple-element.550), kind=kOutput, calls=%fused_computation.229 | convolution fusion | flops 5916061696 | bytes 25575424 | tf_op jit(solution)/vmap(transpose(jvp()))/dot_general | solution.py:20
  390.6 6.6 copy.5
  397.2 69.6 %while.17 = (bf16[1,1,4096,1408]{2,3,1,0:T(8,128)(2,1)}, bf16[1,1,4096,512]{3,2,1,0:T(8,128)(2,1)}, f32[1,88,512]{2,1,0:T(8,128)S(1)}, f32[1,88,512]{2,1,0:T(8,1...) while((bf16[1,1,4096,1408]{2,3,1,0:T(8,128)(2,1)}, ...), condition=%wide.windowed_dot_general_cond_rs.5.clone, body=%wide.windowed_dot_general_body_rs.5.clone.sunk | while | flops 1482432512 | bytes 37945956 | solution.py:9
  467.4 92.0 %while.14 = (bf16[1,1,4096,512]{2,3,1,0:T(8,128)(2,1)}, bf16[1,1,4096,1408]{3,2,1,0:T(8,128)(2,1)}, f32[1,32,1408]{2,1,0:T(8,128)S(1)}, f32[1,32,1408]{2,1,0:T(8...) while((bf16[1,1,4096,512]{2,3,1,0:T(8,128)(2,1)}, ...), condition=%wide.windowed_dot_general_cond_rs.2.clone, body=%wide.windowed_dot_general_body_rs.2.clone.sunk | while | flops 1478762496 | bytes 37945956 | solution.py:21
  472.4 6.4 fusion.323
  482.6 6.4 fusion.325
  495.6 6.4 fusion.323
  505.8 6.4 fusion.325
  518.9 6.4 fusion.323
  529.0 6.4 fusion.325
  542.1 6.4 fusion.323
  552.3 6.4 fusion.325
  559.4 29.2 %fusion.155 = (bf16[1,1,4096,1408]{3,2,1,0:T(8,128)(2,1)}, bf16[1,1,4096,1408]{3,2,1,0:T(8,128)(2,1)}) fusion(f32[4096,1408]{1,0:T(8,128)} %fusion.232, f32[4096,1408]{1,0:T(8,128)} %get-tuple-element.269, bf16[1,1408,512]{2,1,0:T(8,128)(2,1)} %all-gather.33.cloned.1.call-done, bf16[1,1,4096,512]{2,3,1,0:T(8,128)(2,1)} %fusion.222), kind=kOutput, calls=%fused_computation.177 | convolution fusion | flops 5997854720 | bytes 74842112 | tf_op jit(solution)/vmap(transpose(jvp()))/dot_general | solution.py:9
  588.7 12.6 %fusion.196 = bf16[4096,512]{0,1:T(8,128)(2,1)} fusion(bf16[1,1,4096,1408]{3,2,1,0:T(8,128)(2,1)} %get-tuple-element.589, bf16[1,512,1408]{2,1,0:T(8,128)(2,1)S(1)} %copy-done.29), kind=kOutput, calls=%fused_computation.233 | convolution fusion | flops 5905580032 | bytes 17170432 | tf_op jit(solution)/vmap(transpose(jvp()))/dot_general | solution.py:21
  601.4 11.7 %fusion.183 = (bf16[1,1,4096,512]{2,3,1,0:T(8,128)(2,1)}, f32[4096]{0:T(1024)}, bf16[1,1,4096,512]{2,3,1,0:T(8,128)(2,1)}) fusion(bf16[1,4096,512]{1,2,0:T(8,128)(2,1)S(1)} %copy-done.2, f32[4096]{0:T(1024)S(1)} %bitcast.592, bf16[4096,512]{0,1:T(8,128)(2,1)} %fusion.196, bf16[1,512,1408]{2,1,0:T(8,128)(2,1)S(1)} %copy-done.28, ...), kind=kOutput, calls=%fused_computation.226 | convolution fusion | flops 5920256000 | bytes 29786112 | tf_op jit(solution)/vmap(transpose(jvp()))/dot_general | solution.py:20
  613.0 86.9 %while.15 = (bf16[1,1,4096,512]{2,3,1,0:T(8,128)(2,1)}, bf16[1,1,4096,1408]{3,2,1,0:T(8,128)(2,1)}, f32[1,32,1408]{2,1,0:T(8,128)S(1)}, f32[1,32,1408]{2,1,0:T(8...) while((bf16[1,1,4096,512]{2,3,1,0:T(8,128)(2,1)}, ...), condition=%wide.windowed_dot_general_cond_rs.3.clone, body=%wide.windowed_dot_general_body_rs.3.clone.sunk | while | flops 1478762496 | bytes 37945956 | solution.py:21
  618.3 6.4 fusion.331
  628.5 6.4 fusion.333
  640.0 6.4 fusion.331
  650.1 6.4 fusion.333
  661.6 6.4 fusion.331
  671.8 6.4 fusion.333
  683.3 6.4 fusion.331
  693.4 6.4 fusion.333
  700.0 86.6 %while.12 = (bf16[1,1,4096,512]{2,3,1,0:T(8,128)(2,1)}, bf16[1,1,4096,1408]{3,2,1,0:T(8,128)(2,1)}, f32[1,32,1408]{2,1,0:T(8,128)S(1)}, f32[1,32,1408]{2,1,0:T(8...) while((bf16[1,1,4096,512]{2,3,1,0:T(8,128)(2,1)}, ...), condition=%wide.windowed_dot_general_cond_rs.clone, body=%wide.windowed_dot_general_body_rs.clone.sunk | while | flops 1478762496 | bytes 37945956 | solution.py:20
  705.0 6.4 fusion.307
  715.1 6.4 fusion.309
  726.6 6.4 fusion.307
  736.8 6.4 fusion.309
  748.3 6.4 fusion.307
  758.5 6.4 fusion.309
  770.0 6.4 fusion.307
  780.1 6.4 fusion.309
  786.7 86.6 %while.13 = (bf16[1,1,4096,512]{2,3,1,0:T(8,128)(2,1)}, bf16[1,1,4096,1408]{3,2,1,0:T(8,128)(2,1)}, f32[1,32,1408]{2,1,0:T(8,128)S(1)}, f32[1,32,1408]{2,1,0:T(8...) while((bf16[1,1,4096,512]{2,3,1,0:T(8,128)(2,1)}, ...), condition=%wide.windowed_dot_general_cond_rs.1.clone, body=%wide.windowed_dot_general_body_rs.1.clone.sunk | while | flops 1478762496 | bytes 37945956 | solution.py:20
  791.7 6.4 fusion.315
  801.8 6.4 fusion.317
  813.3 6.4 fusion.315
  823.5 6.4 fusion.317
  835.0 6.4 fusion.315
  845.2 6.4 fusion.317
  856.7 6.4 fusion.315
  866.8 6.4 fusion.317
  873.5 7.5 fusion.221
  881.0 6.5 copy.6
  (451 shorter events, 262.5 us)
Async XLA Ops:
  7.2 41.9 %all-gather.37.cloned.1.call-start = ((), (), s32[]{:S(2)}) async-start(), calls=%async_computation.4 | async-start | bytes 1531904 | tf_op jit(solution)/vmap(jvp())/squeeze | solution.py:27
  8.9 75.9 %all-gather.29.cloned.1.call-start = ((), (), s32[]{:S(2)}) async-start(), calls=%async_computation | async-start | bytes 1531904 | tf_op jit(solution)/vmap(jvp())/squeeze | solution.py:27
  10.7 109.9 %all-gather.31.cloned.1.call-start = ((), (), s32[]{:S(2)}) async-start(), calls=%async_computation.1 | async-start | bytes 1531904 | tf_op jit(solution)/vmap(jvp())/squeeze | solution.py:27
  12.4 143.8 %all-gather.33.cloned.1.call-start = ((), (), s32[]{:S(2)}) async-start(), calls=%async_computation.2 | async-start | bytes 1531904 | tf_op jit(solution)/vmap(jvp())/squeeze | solution.py:27
  13.1 178.8 %all-gather.39.cloned.1.call-start = ((), (), s32[]{:S(2)}) async-start(), calls=%async_computation.5 | async-start | bytes 1531904 | tf_op jit(solution)/vmap(jvp())/squeeze | solution.py:27
  13.7 213.8 %all-gather.35.cloned.1.call-start = ((), (), s32[]{:S(2)}) async-start(), calls=%async_computation.3 | async-start | bytes 1531904 | tf_op jit(solution)/vmap(jvp())/squeeze | solution.py:27
  366.1 522.5 %collective-permute-start.28 = (f32[1,88,512]{2,1,0:T(8,128)}, f32[1,88,512]{2,1,0:T(8,128)}, u32[]{:S(2)}, u32[]{:S(2)}) collective-permute-start(f32[1,88,512]{2,1,0:T(8,128)} %get-tuple-element.45), channel_id=41, source_target_pairs={{0,1},{1,2},{2,3},{3,4},{4,5},{5,6},{6,7},{7,8},{8,9},{9,10},{10,1... | collective-permute-start | bytes 540680 | tf_op jit(solution)/vmap(transpose(jvp()))/dot_general | solution.py:9
  466.7 422.8 %collective-permute-start.29 = (f32[1,88,512]{2,1,0:T(8,128)}, f32[1,88,512]{2,1,0:T(8,128)}, u32[]{:S(2)}, u32[]{:S(2)}) collective-permute-start(f32[1,88,512]{2,1,0:T(8,128)} %get-tuple-element.47), channel_id=47, source_target_pairs={{0,1},{1,2},{2,3},{3,4},{4,5},{5,6},{6,7},{7,8},{8,9},{9,10},{10,1... | collective-permute-start | bytes 540680 | tf_op jit(solution)/vmap(transpose(jvp()))/dot_general | solution.py:9
  467.4 12.1 %collective-permute-start.8 = (f32[1,32,1408]{2,1,0:T(8,128)S(1)}, f32[1,32,1408]{2,1,0:T(8,128)S(1)}, u32[]{:S(2)}, u32[]{:S(2)}) collective-permute-start(f32[1,32,1408]{2,1,0:T(8,128)S(1)} %broadcast_select_fusion.28), channel_id=26, source_target_pairs={{0,1},{1,2},{2,3},{3,4},{4,5},{5,6},{6,7},{7,8},{8,9},{9,10},{10,1... | collective-permute-start | bytes 540680 | tf_op jit(solution)/vmap(transpose(jvp()))/dot_general | solution.py:21
  467.5 12.0 %collective-permute-start.9 = (f32[1,32,1408]{2,1,0:T(8,128)S(1)}, f32[1,32,1408]{2,1,0:T(8,128)S(1)}, u32[]{:S(2)}, u32[]{:S(2)}) collective-permute-start(f32[1,32,1408]{2,1,0:T(8,128)S(1)} %broadcast_select_fusion.29), channel_id=25, source_target_pairs={{0,15},{1,0},{2,1},{3,2},{4,3},{5,4},{6,5},{7,6},{8,7},{9,8},{10,9... | collective-permute-start | bytes 540680 | tf_op jit(solution)/vmap(transpose(jvp()))/dot_general | solution.py:21
  479.6 9.4 %collective-permute-start.10 = (f32[1,32,1408]{2,1,0:T(8,128)S(1)}, f32[1,32,1408]{2,1,0:T(8,128)S(1)}, u32[]{:S(2)}, u32[]{:S(2)}) collective-permute-start(f32[1,32,1408]{2,1,0:T(8,128)S(1)} %get-tuple-element.479), channel_id=28, source_target_pairs={{0,1},{1,2},{2,3},{3,4},{4,5},{5,6},{6,7},{7,8},{8,9},{9,10},{10,1... | collective-permute-start | bytes 540680 | tf_op jit(solution)/vmap(transpose(jvp()))/dot_general | solution.py:21
  479.6 9.4 %collective-permute-start.11 = (f32[1,32,1408]{2,1,0:T(8,128)S(1)}, f32[1,32,1408]{2,1,0:T(8,128)S(1)}, u32[]{:S(2)}, u32[]{:S(2)}) collective-permute-start(f32[1,32,1408]{2,1,0:T(8,128)S(1)} %get-tuple-element.480), channel_id=27, source_target_pairs={{0,15},{1,0},{2,1},{3,2},{4,3},{5,4},{6,5},{7,6},{8,7},{9,8},{10,9... | collective-permute-start | bytes 540680 | tf_op jit(solution)/vmap(transpose(jvp()))/dot_general | solution.py:21
  490.7 12.1 %collective-permute-start.8 = (f32[1,32,1408]{2,1,0:T(8,128)S(1)}, f32[1,32,1408]{2,1,0:T(8,128)S(1)}, u32[]{:S(2)}, u32[]{:S(2)}) collective-permute-start(f32[1,32,1408]{2,1,0:T(8,128)S(1)} %broadcast_select_fusion.28), channel_id=26, source_target_pairs={{0,1},{1,2},{2,3},{3,4},{4,5},{5,6},{6,7},{7,8},{8,9},{9,10},{10,1... | collective-permute-start | bytes 540680 | tf_op jit(solution)/vmap(transpose(jvp()))/dot_general | solution.py:21
  490.8 12.0 %collective-permute-start.9 = (f32[1,32,1408]{2,1,0:T(8,128)S(1)}, f32[1,32,1408]{2,1,0:T(8,128)S(1)}, u32[]{:S(2)}, u32[]{:S(2)}) collective-permute-start(f32[1,32,1408]{2,1,0:T(8,128)S(1)} %broadcast_select_fusion.29), channel_id=25, source_target_pairs={{0,15},{1,0},{2,1},{3,2},{4,3},{5,4},{6,5},{7,6},{8,7},{9,8},{10,9... | collective-permute-start | bytes 540680 | tf_op jit(solution)/vmap(transpose(jvp()))/dot_general | solution.py:21
  502.8 9.4 %collective-permute-start.10 = (f32[1,32,1408]{2,1,0:T(8,128)S(1)}, f32[1,32,1408]{2,1,0:T(8,128)S(1)}, u32[]{:S(2)}, u32[]{:S(2)}) collective-permute-start(f32[1,32,1408]{2,1,0:T(8,128)S(1)} %get-tuple-element.479), channel_id=28, source_target_pairs={{0,1},{1,2},{2,3},{3,4},{4,5},{5,6},{6,7},{7,8},{8,9},{9,10},{10,1... | collective-permute-start | bytes 540680 | tf_op jit(solution)/vmap(transpose(jvp()))/dot_general | solution.py:21
  502.9 9.4 %collective-permute-start.11 = (f32[1,32,1408]{2,1,0:T(8,128)S(1)}, f32[1,32,1408]{2,1,0:T(8,128)S(1)}, u32[]{:S(2)}, u32[]{:S(2)}) collective-permute-start(f32[1,32,1408]{2,1,0:T(8,128)S(1)} %get-tuple-element.480), channel_id=27, source_target_pairs={{0,15},{1,0},{2,1},{3,2},{4,3},{5,4},{6,5},{7,6},{8,7},{9,8},{10,9... | collective-permute-start | bytes 540680 | tf_op jit(solution)/vmap(transpose(jvp()))/dot_general | solution.py:21
  513.9 12.1 %collective-permute-start.8 = (f32[1,32,1408]{2,1,0:T(8,128)S(1)}, f32[1,32,1408]{2,1,0:T(8,128)S(1)}, u32[]{:S(2)}, u32[]{:S(2)}) collective-permute-start(f32[1,32,1408]{2,1,0:T(8,128)S(1)} %broadcast_select_fusion.28), channel_id=26, source_target_pairs={{0,1},{1,2},{2,3},{3,4},{4,5},{5,6},{6,7},{7,8},{8,9},{9,10},{10,1... | collective-permute-start | bytes 540680 | tf_op jit(solution)/vmap(transpose(jvp()))/dot_general | solution.py:21
  514.0 12.0 %collective-permute-start.9 = (f32[1,32,1408]{2,1,0:T(8,128)S(1)}, f32[1,32,1408]{2,1,0:T(8,128)S(1)}, u32[]{:S(2)}, u32[]{:S(2)}) collective-permute-start(f32[1,32,1408]{2,1,0:T(8,128)S(1)} %broadcast_select_fusion.29), channel_id=25, source_target_pairs={{0,15},{1,0},{2,1},{3,2},{4,3},{5,4},{6,5},{7,6},{8,7},{9,8},{10,9... | collective-permute-start | bytes 540680 | tf_op jit(solution)/vmap(transpose(jvp()))/dot_general | solution.py:21
  526.0 9.4 %collective-permute-start.10 = (f32[1,32,1408]{2,1,0:T(8,128)S(1)}, f32[1,32,1408]{2,1,0:T(8,128)S(1)}, u32[]{:S(2)}, u32[]{:S(2)}) collective-permute-start(f32[1,32,1408]{2,1,0:T(8,128)S(1)} %get-tuple-element.479), channel_id=28, source_target_pairs={{0,1},{1,2},{2,3},{3,4},{4,5},{5,6},{6,7},{7,8},{8,9},{9,10},{10,1... | collective-permute-start | bytes 540680 | tf_op jit(solution)/vmap(transpose(jvp()))/dot_general | solution.py:21
  526.1 9.4 %collective-permute-start.11 = (f32[1,32,1408]{2,1,0:T(8,128)S(1)}, f32[1,32,1408]{2,1,0:T(8,128)S(1)}, u32[]{:S(2)}, u32[]{:S(2)}) collective-permute-start(f32[1,32,1408]{2,1,0:T(8,128)S(1)} %get-tuple-element.480), channel_id=27, source_target_pairs={{0,15},{1,0},{2,1},{3,2},{4,3},{5,4},{6,5},{7,6},{8,7},{9,8},{10,9... | collective-permute-start | bytes 540680 | tf_op jit(solution)/vmap(transpose(jvp()))/dot_general | solution.py:21
  537.1 12.1 %collective-permute-start.8 = (f32[1,32,1408]{2,1,0:T(8,128)S(1)}, f32[1,32,1408]{2,1,0:T(8,128)S(1)}, u32[]{:S(2)}, u32[]{:S(2)}) collective-permute-start(f32[1,32,1408]{2,1,0:T(8,128)S(1)} %broadcast_select_fusion.28), channel_id=26, source_target_pairs={{0,1},{1,2},{2,3},{3,4},{4,5},{5,6},{6,7},{7,8},{8,9},{9,10},{10,1... | collective-permute-start | bytes 540680 | tf_op jit(solution)/vmap(transpose(jvp()))/dot_general | solution.py:21
  537.2 12.0 %collective-permute-start.9 = (f32[1,32,1408]{2,1,0:T(8,128)S(1)}, f32[1,32,1408]{2,1,0:T(8,128)S(1)}, u32[]{:S(2)}, u32[]{:S(2)}) collective-permute-start(f32[1,32,1408]{2,1,0:T(8,128)S(1)} %broadcast_select_fusion.29), channel_id=25, source_target_pairs={{0,15},{1,0},{2,1},{3,2},{4,3},{5,4},{6,5},{7,6},{8,7},{9,8},{10,9... | collective-permute-start | bytes 540680 | tf_op jit(solution)/vmap(transpose(jvp()))/dot_general | solution.py:21
  549.3 9.4 %collective-permute-start.10 = (f32[1,32,1408]{2,1,0:T(8,128)S(1)}, f32[1,32,1408]{2,1,0:T(8,128)S(1)}, u32[]{:S(2)}, u32[]{:S(2)}) collective-permute-start(f32[1,32,1408]{2,1,0:T(8,128)S(1)} %get-tuple-element.479), channel_id=28, source_target_pairs={{0,1},{1,2},{2,3},{3,4},{4,5},{5,6},{6,7},{7,8},{8,9},{9,10},{10,1... | collective-permute-start | bytes 540680 | tf_op jit(solution)/vmap(transpose(jvp()))/dot_general | solution.py:21
  559.4 328.1 %collective-permute-start.26 = (f32[1,32,1408]{2,1,0:T(8,128)}, f32[1,32,1408]{2,1,0:T(8,128)}, u32[]{:S(2)}, u32[]{:S(2)}) collective-permute-start(f32[1,32,1408]{2,1,0:T(8,128)} %get-tuple-element.41), channel_id=29, source_target_pairs={{0,1},{1,2},{2,3},{3,4},{4,5},{5,6},{6,7},{7,8},{8,9},{9,10},{10,1... | collective-permute-start | bytes 540680 | tf_op jit(solution)/vmap(transpose(jvp()))/dot_general | solution.py:21
  613.3 12.0 %collective-permute-start.12 = (f32[1,32,1408]{2,1,0:T(8,128)S(1)}, f32[1,32,1408]{2,1,0:T(8,128)S(1)}, u32[]{:S(2)}, u32[]{:S(2)}) collective-permute-start(f32[1,32,1408]{2,1,0:T(8,128)S(1)} %broadcast_select_fusion.30), channel_id=32, source_target_pairs={{0,1},{1,2},{2,3},{3,4},{4,5},{5,6},{6,7},{7,8},{8,9},{9,10},{10,1... | collective-permute-start | bytes 540680 | tf_op jit(solution)/vmap(transpose(jvp()))/dot_general | solution.py:21
  613.4 12.0 %collective-permute-start.13 = (f32[1,32,1408]{2,1,0:T(8,128)S(1)}, f32[1,32,1408]{2,1,0:T(8,128)S(1)}, u32[]{:S(2)}, u32[]{:S(2)}) collective-permute-start(f32[1,32,1408]{2,1,0:T(8,128)S(1)} %broadcast_select_fusion.31), channel_id=31, source_target_pairs={{0,15},{1,0},{2,1},{3,2},{4,3},{5,4},{6,5},{7,6},{8,7},{9,8},{10,9... | collective-permute-start | bytes 540680 | tf_op jit(solution)/vmap(transpose(jvp()))/dot_general | solution.py:21
  625.5 9.4 %collective-permute-start.14 = (f32[1,32,1408]{2,1,0:T(8,128)S(1)}, f32[1,32,1408]{2,1,0:T(8,128)S(1)}, u32[]{:S(2)}, u32[]{:S(2)}) collective-permute-start(f32[1,32,1408]{2,1,0:T(8,128)S(1)} %get-tuple-element.488), channel_id=34, source_target_pairs={{0,1},{1,2},{2,3},{3,4},{4,5},{5,6},{6,7},{7,8},{8,9},{9,10},{10,1... | collective-permute-start | bytes 540680 | tf_op jit(solution)/vmap(transpose(jvp()))/dot_general | solution.py:21
  625.5 9.4 %collective-permute-start.15 = (f32[1,32,1408]{2,1,0:T(8,128)S(1)}, f32[1,32,1408]{2,1,0:T(8,128)S(1)}, u32[]{:S(2)}, u32[]{:S(2)}) collective-permute-start(f32[1,32,1408]{2,1,0:T(8,128)S(1)} %get-tuple-element.489), channel_id=33, source_target_pairs={{0,15},{1,0},{2,1},{3,2},{4,3},{5,4},{6,5},{7,6},{8,7},{9,8},{10,9... | collective-permute-start | bytes 540680 | tf_op jit(solution)/vmap(transpose(jvp()))/dot_general | solution.py:21
  635.0 12.0 %collective-permute-start.12 = (f32[1,32,1408]{2,1,0:T(8,128)S(1)}, f32[1,32,1408]{2,1,0:T(8,128)S(1)}, u32[]{:S(2)}, u32[]{:S(2)}) collective-permute-start(f32[1,32,1408]{2,1,0:T(8,128)S(1)} %broadcast_select_fusion.30), channel_id=32, source_target_pairs={{0,1},{1,2},{2,3},{3,4},{4,5},{5,6},{6,7},{7,8},{8,9},{9,10},{10,1... | collective-permute-start | bytes 540680 | tf_op jit(solution)/vmap(transpose(jvp()))/dot_general | solution.py:21
  635.1 12.0 %collective-permute-start.13 = (f32[1,32,1408]{2,1,0:T(8,128)S(1)}, f32[1,32,1408]{2,1,0:T(8,128)S(1)}, u32[]{:S(2)}, u32[]{:S(2)}) collective-permute-start(f32[1,32,1408]{2,1,0:T(8,128)S(1)} %broadcast_select_fusion.31), channel_id=31, source_target_pairs={{0,15},{1,0},{2,1},{3,2},{4,3},{5,4},{6,5},{7,6},{8,7},{9,8},{10,9... | collective-permute-start | bytes 540680 | tf_op jit(solution)/vmap(transpose(jvp()))/dot_general | solution.py:21
  647.1 9.4 %collective-permute-start.14 = (f32[1,32,1408]{2,1,0:T(8,128)S(1)}, f32[1,32,1408]{2,1,0:T(8,128)S(1)}, u32[]{:S(2)}, u32[]{:S(2)}) collective-permute-start(f32[1,32,1408]{2,1,0:T(8,128)S(1)} %get-tuple-element.488), channel_id=34, source_target_pairs={{0,1},{1,2},{2,3},{3,4},{4,5},{5,6},{6,7},{7,8},{8,9},{9,10},{10,1... | collective-permute-start | bytes 540680 | tf_op jit(solution)/vmap(transpose(jvp()))/dot_general | solution.py:21
  647.2 9.4 %collective-permute-start.15 = (f32[1,32,1408]{2,1,0:T(8,128)S(1)}, f32[1,32,1408]{2,1,0:T(8,128)S(1)}, u32[]{:S(2)}, u32[]{:S(2)}) collective-permute-start(f32[1,32,1408]{2,1,0:T(8,128)S(1)} %get-tuple-element.489), channel_id=33, source_target_pairs={{0,15},{1,0},{2,1},{3,2},{4,3},{5,4},{6,5},{7,6},{8,7},{9,8},{10,9... | collective-permute-start | bytes 540680 | tf_op jit(solution)/vmap(transpose(jvp()))/dot_general | solution.py:21
  656.7 12.0 %collective-permute-start.12 = (f32[1,32,1408]{2,1,0:T(8,128)S(1)}, f32[1,32,1408]{2,1,0:T(8,128)S(1)}, u32[]{:S(2)}, u32[]{:S(2)}) collective-permute-start(f32[1,32,1408]{2,1,0:T(8,128)S(1)} %broadcast_select_fusion.30), channel_id=32, source_target_pairs={{0,1},{1,2},{2,3},{3,4},{4,5},{5,6},{6,7},{7,8},{8,9},{9,10},{10,1... | collective-permute-start | bytes 540680 | tf_op jit(solution)/vmap(transpose(jvp()))/dot_general | solution.py:21
  656.8 12.0 %collective-permute-start.13 = (f32[1,32,1408]{2,1,0:T(8,128)S(1)}, f32[1,32,1408]{2,1,0:T(8,128)S(1)}, u32[]{:S(2)}, u32[]{:S(2)}) collective-permute-start(f32[1,32,1408]{2,1,0:T(8,128)S(1)} %broadcast_select_fusion.31), channel_id=31, source_target_pairs={{0,15},{1,0},{2,1},{3,2},{4,3},{5,4},{6,5},{7,6},{8,7},{9,8},{10,9... | collective-permute-start | bytes 540680 | tf_op jit(solution)/vmap(transpose(jvp()))/dot_general | solution.py:21
  668.8 9.4 %collective-permute-start.14 = (f32[1,32,1408]{2,1,0:T(8,128)S(1)}, f32[1,32,1408]{2,1,0:T(8,128)S(1)}, u32[]{:S(2)}, u32[]{:S(2)}) collective-permute-start(f32[1,32,1408]{2,1,0:T(8,128)S(1)} %get-tuple-element.488), channel_id=34, source_target_pairs={{0,1},{1,2},{2,3},{3,4},{4,5},{5,6},{6,7},{7,8},{8,9},{9,10},{10,1... | collective-permute-start | bytes 540680 | tf_op jit(solution)/vmap(transpose(jvp()))/dot_general | solution.py:21
  678.3 12.0 %collective-permute-start.12 = (f32[1,32,1408]{2,1,0:T(8,128)S(1)}, f32[1,32,1408]{2,1,0:T(8,128)S(1)}, u32[]{:S(2)}, u32[]{:S(2)}) collective-permute-start(f32[1,32,1408]{2,1,0:T(8,128)S(1)} %broadcast_select_fusion.30), channel_id=32, source_target_pairs={{0,1},{1,2},{2,3},{3,4},{4,5},{5,6},{6,7},{7,8},{8,9},{9,10},{10,1... | collective-permute-start | bytes 540680 | tf_op jit(solution)/vmap(transpose(jvp()))/dot_general | solution.py:21
  678.4 12.0 %collective-permute-start.13 = (f32[1,32,1408]{2,1,0:T(8,128)S(1)}, f32[1,32,1408]{2,1,0:T(8,128)S(1)}, u32[]{:S(2)}, u32[]{:S(2)}) collective-permute-start(f32[1,32,1408]{2,1,0:T(8,128)S(1)} %broadcast_select_fusion.31), channel_id=31, source_target_pairs={{0,15},{1,0},{2,1},{3,2},{4,3},{5,4},{6,5},{7,6},{8,7},{9,8},{10,9... | collective-permute-start | bytes 540680 | tf_op jit(solution)/vmap(transpose(jvp()))/dot_general | solution.py:21
  690.4 9.4 %collective-permute-start.14 = (f32[1,32,1408]{2,1,0:T(8,128)S(1)}, f32[1,32,1408]{2,1,0:T(8,128)S(1)}, u32[]{:S(2)}, u32[]{:S(2)}) collective-permute-start(f32[1,32,1408]{2,1,0:T(8,128)S(1)} %get-tuple-element.488), channel_id=34, source_target_pairs={{0,1},{1,2},{2,3},{3,4},{4,5},{5,6},{6,7},{7,8},{8,9},{9,10},{10,1... | collective-permute-start | bytes 540680 | tf_op jit(solution)/vmap(transpose(jvp()))/dot_general | solution.py:21
  690.5 9.4 %collective-permute-start.15 = (f32[1,32,1408]{2,1,0:T(8,128)S(1)}, f32[1,32,1408]{2,1,0:T(8,128)S(1)}, u32[]{:S(2)}, u32[]{:S(2)}) collective-permute-start(f32[1,32,1408]{2,1,0:T(8,128)S(1)} %get-tuple-element.489), channel_id=33, source_target_pairs={{0,15},{1,0},{2,1},{3,2},{4,3},{5,4},{6,5},{7,6},{8,7},{9,8},{10,9... | collective-permute-start | bytes 540680 | tf_op jit(solution)/vmap(transpose(jvp()))/dot_general | solution.py:21
  700.0 12.1 %collective-permute-start = (f32[1,32,1408]{2,1,0:T(8,128)S(1)}, f32[1,32,1408]{2,1,0:T(8,128)S(1)}, u32[]{:S(2)}, u32[]{:S(2)}) collective-permute-start(f32[1,32,1408]{2,1,0:T(8,128)S(1)} %broadcast_select_fusion.24), channel_id=14, source_target_pairs={{0,1},{1,2},{2,3},{3,4},{4,5},{5,6},{6,7},{7,8},{8,9},{9,10},{10,1... | collective-permute-start | bytes 540680 | tf_op jit(solution)/vmap(transpose(jvp()))/dot_general | solution.py:20
  700.1 12.0 %collective-permute-start.1 = (f32[1,32,1408]{2,1,0:T(8,128)S(1)}, f32[1,32,1408]{2,1,0:T(8,128)S(1)}, u32[]{:S(2)}, u32[]{:S(2)}) collective-permute-start(f32[1,32,1408]{2,1,0:T(8,128)S(1)} %broadcast_select_fusion.25), channel_id=13, source_target_pairs={{0,15},{1,0},{2,1},{3,2},{4,3},{5,4},{6,5},{7,6},{8,7},{9,8},{10,9... | collective-permute-start | bytes 540680 | tf_op jit(solution)/vmap(transpose(jvp()))/dot_general | solution.py:20
  712.1 9.4 %collective-permute-start.2 = (f32[1,32,1408]{2,1,0:T(8,128)S(1)}, f32[1,32,1408]{2,1,0:T(8,128)S(1)}, u32[]{:S(2)}, u32[]{:S(2)}) collective-permute-start(f32[1,32,1408]{2,1,0:T(8,128)S(1)} %get-tuple-element.461), channel_id=16, source_target_pairs={{0,1},{1,2},{2,3},{3,4},{4,5},{5,6},{6,7},{7,8},{8,9},{9,10},{10,1... | collective-permute-start | bytes 540680 | tf_op jit(solution)/vmap(transpose(jvp()))/dot_general | solution.py:20
  721.7 12.0 %collective-permute-start = (f32[1,32,1408]{2,1,0:T(8,128)S(1)}, f32[1,32,1408]{2,1,0:T(8,128)S(1)}, u32[]{:S(2)}, u32[]{:S(2)}) collective-permute-start(f32[1,32,1408]{2,1,0:T(8,128)S(1)} %broadcast_select_fusion.24), channel_id=14, source_target_pairs={{0,1},{1,2},{2,3},{3,4},{4,5},{5,6},{6,7},{7,8},{8,9},{9,10},{10,1... | collective-permute-start | bytes 540680 | tf_op jit(solution)/vmap(transpose(jvp()))/dot_general | solution.py:20
  721.8 12.0 %collective-permute-start.1 = (f32[1,32,1408]{2,1,0:T(8,128)S(1)}, f32[1,32,1408]{2,1,0:T(8,128)S(1)}, u32[]{:S(2)}, u32[]{:S(2)}) collective-permute-start(f32[1,32,1408]{2,1,0:T(8,128)S(1)} %broadcast_select_fusion.25), channel_id=13, source_target_pairs={{0,15},{1,0},{2,1},{3,2},{4,3},{5,4},{6,5},{7,6},{8,7},{9,8},{10,9... | collective-permute-start | bytes 540680 | tf_op jit(solution)/vmap(transpose(jvp()))/dot_general | solution.py:20
  733.8 9.4 %collective-permute-start.2 = (f32[1,32,1408]{2,1,0:T(8,128)S(1)}, f32[1,32,1408]{2,1,0:T(8,128)S(1)}, u32[]{:S(2)}, u32[]{:S(2)}) collective-permute-start(f32[1,32,1408]{2,1,0:T(8,128)S(1)} %get-tuple-element.461), channel_id=16, source_target_pairs={{0,1},{1,2},{2,3},{3,4},{4,5},{5,6},{6,7},{7,8},{8,9},{9,10},{10,1... | collective-permute-start | bytes 540680 | tf_op jit(solution)/vmap(transpose(jvp()))/dot_general | solution.py:20
  743.3 12.0 %collective-permute-start = (f32[1,32,1408]{2,1,0:T(8,128)S(1)}, f32[1,32,1408]{2,1,0:T(8,128)S(1)}, u32[]{:S(2)}, u32[]{:S(2)}) collective-permute-start(f32[1,32,1408]{2,1,0:T(8,128)S(1)} %broadcast_select_fusion.24), channel_id=14, source_target_pairs={{0,1},{1,2},{2,3},{3,4},{4,5},{5,6},{6,7},{7,8},{8,9},{9,10},{10,1... | collective-permute-start | bytes 540680 | tf_op jit(solution)/vmap(transpose(jvp()))/dot_general | solution.py:20
  743.4 12.0 %collective-permute-start.1 = (f32[1,32,1408]{2,1,0:T(8,128)S(1)}, f32[1,32,1408]{2,1,0:T(8,128)S(1)}, u32[]{:S(2)}, u32[]{:S(2)}) collective-permute-start(f32[1,32,1408]{2,1,0:T(8,128)S(1)} %broadcast_select_fusion.25), channel_id=13, source_target_pairs={{0,15},{1,0},{2,1},{3,2},{4,3},{5,4},{6,5},{7,6},{8,7},{9,8},{10,9... | collective-permute-start | bytes 540680 | tf_op jit(solution)/vmap(transpose(jvp()))/dot_general | solution.py:20
  755.5 9.4 %collective-permute-start.2 = (f32[1,32,1408]{2,1,0:T(8,128)S(1)}, f32[1,32,1408]{2,1,0:T(8,128)S(1)}, u32[]{:S(2)}, u32[]{:S(2)}) collective-permute-start(f32[1,32,1408]{2,1,0:T(8,128)S(1)} %get-tuple-element.461), channel_id=16, source_target_pairs={{0,1},{1,2},{2,3},{3,4},{4,5},{5,6},{6,7},{7,8},{8,9},{9,10},{10,1... | collective-permute-start | bytes 540680 | tf_op jit(solution)/vmap(transpose(jvp()))/dot_general | solution.py:20
  765.0 12.0 %collective-permute-start = (f32[1,32,1408]{2,1,0:T(8,128)S(1)}, f32[1,32,1408]{2,1,0:T(8,128)S(1)}, u32[]{:S(2)}, u32[]{:S(2)}) collective-permute-start(f32[1,32,1408]{2,1,0:T(8,128)S(1)} %broadcast_select_fusion.24), channel_id=14, source_target_pairs={{0,1},{1,2},{2,3},{3,4},{4,5},{5,6},{6,7},{7,8},{8,9},{9,10},{10,1... | collective-permute-start | bytes 540680 | tf_op jit(solution)/vmap(transpose(jvp()))/dot_general | solution.py:20
  765.1 12.0 %collective-permute-start.1 = (f32[1,32,1408]{2,1,0:T(8,128)S(1)}, f32[1,32,1408]{2,1,0:T(8,128)S(1)}, u32[]{:S(2)}, u32[]{:S(2)}) collective-permute-start(f32[1,32,1408]{2,1,0:T(8,128)S(1)} %broadcast_select_fusion.25), channel_id=13, source_target_pairs={{0,15},{1,0},{2,1},{3,2},{4,3},{5,4},{6,5},{7,6},{8,7},{9,8},{10,9... | collective-permute-start | bytes 540680 | tf_op jit(solution)/vmap(transpose(jvp()))/dot_general | solution.py:20
  777.1 9.4 %collective-permute-start.2 = (f32[1,32,1408]{2,1,0:T(8,128)S(1)}, f32[1,32,1408]{2,1,0:T(8,128)S(1)}, u32[]{:S(2)}, u32[]{:S(2)}) collective-permute-start(f32[1,32,1408]{2,1,0:T(8,128)S(1)} %get-tuple-element.461), channel_id=16, source_target_pairs={{0,1},{1,2},{2,3},{3,4},{4,5},{5,6},{6,7},{7,8},{8,9},{9,10},{10,1... | collective-permute-start | bytes 540680 | tf_op jit(solution)/vmap(transpose(jvp()))/dot_general | solution.py:20
  786.7 12.1 %collective-permute-start.4 = (f32[1,32,1408]{2,1,0:T(8,128)S(1)}, f32[1,32,1408]{2,1,0:T(8,128)S(1)}, u32[]{:S(2)}, u32[]{:S(2)}) collective-permute-start(f32[1,32,1408]{2,1,0:T(8,128)S(1)} %broadcast_select_fusion.26), channel_id=20, source_target_pairs={{0,1},{1,2},{2,3},{3,4},{4,5},{5,6},{6,7},{7,8},{8,9},{9,10},{10,1... | collective-permute-start | bytes 540680 | tf_op jit(solution)/vmap(transpose(jvp()))/dot_general | solution.py:20
  786.8 12.0 %collective-permute-start.5 = (f32[1,32,1408]{2,1,0:T(8,128)S(1)}, f32[1,32,1408]{2,1,0:T(8,128)S(1)}, u32[]{:S(2)}, u32[]{:S(2)}) collective-permute-start(f32[1,32,1408]{2,1,0:T(8,128)S(1)} %broadcast_select_fusion.27), channel_id=19, source_target_pairs={{0,15},{1,0},{2,1},{3,2},{4,3},{5,4},{6,5},{7,6},{8,7},{9,8},{10,9... | collective-permute-start | bytes 540680 | tf_op jit(solution)/vmap(transpose(jvp()))/dot_general | solution.py:20
  798.8 9.4 %collective-permute-start.6 = (f32[1,32,1408]{2,1,0:T(8,128)S(1)}, f32[1,32,1408]{2,1,0:T(8,128)S(1)}, u32[]{:S(2)}, u32[]{:S(2)}) collective-permute-start(f32[1,32,1408]{2,1,0:T(8,128)S(1)} %get-tuple-element.470), channel_id=22, source_target_pairs={{0,1},{1,2},{2,3},{3,4},{4,5},{5,6},{6,7},{7,8},{8,9},{9,10},{10,1... | collective-permute-start | bytes 540680 | tf_op jit(solution)/vmap(transpose(jvp()))/dot_general | solution.py:20
  808.4 12.0 %collective-permute-start.4 = (f32[1,32,1408]{2,1,0:T(8,128)S(1)}, f32[1,32,1408]{2,1,0:T(8,128)S(1)}, u32[]{:S(2)}, u32[]{:S(2)}) collective-permute-start(f32[1,32,1408]{2,1,0:T(8,128)S(1)} %broadcast_select_fusion.26), channel_id=20, source_target_pairs={{0,1},{1,2},{2,3},{3,4},{4,5},{5,6},{6,7},{7,8},{8,9},{9,10},{10,1... | collective-permute-start | bytes 540680 | tf_op jit(solution)/vmap(transpose(jvp()))/dot_general | solution.py:20
  808.5 12.0 %collective-permute-start.5 = (f32[1,32,1408]{2,1,0:T(8,128)S(1)}, f32[1,32,1408]{2,1,0:T(8,128)S(1)}, u32[]{:S(2)}, u32[]{:S(2)}) collective-permute-start(f32[1,32,1408]{2,1,0:T(8,128)S(1)} %broadcast_select_fusion.27), channel_id=19, source_target_pairs={{0,15},{1,0},{2,1},{3,2},{4,3},{5,4},{6,5},{7,6},{8,7},{9,8},{10,9... | collective-permute-start | bytes 540680 | tf_op jit(solution)/vmap(transpose(jvp()))/dot_general | solution.py:20
  820.5 9.4 %collective-permute-start.6 = (f32[1,32,1408]{2,1,0:T(8,128)S(1)}, f32[1,32,1408]{2,1,0:T(8,128)S(1)}, u32[]{:S(2)}, u32[]{:S(2)}) collective-permute-start(f32[1,32,1408]{2,1,0:T(8,128)S(1)} %get-tuple-element.470), channel_id=22, source_target_pairs={{0,1},{1,2},{2,3},{3,4},{4,5},{5,6},{6,7},{7,8},{8,9},{9,10},{10,1... | collective-permute-start | bytes 540680 | tf_op jit(solution)/vmap(transpose(jvp()))/dot_general | solution.py:20
  830.0 12.0 %collective-permute-start.4 = (f32[1,32,1408]{2,1,0:T(8,128)S(1)}, f32[1,32,1408]{2,1,0:T(8,128)S(1)}, u32[]{:S(2)}, u32[]{:S(2)}) collective-permute-start(f32[1,32,1408]{2,1,0:T(8,128)S(1)} %broadcast_select_fusion.26), channel_id=20, source_target_pairs={{0,1},{1,2},{2,3},{3,4},{4,5},{5,6},{6,7},{7,8},{8,9},{9,10},{10,1... | collective-permute-start | bytes 540680 | tf_op jit(solution)/vmap(transpose(jvp()))/dot_general | solution.py:20
  830.1 12.0 %collective-permute-start.5 = (f32[1,32,1408]{2,1,0:T(8,128)S(1)}, f32[1,32,1408]{2,1,0:T(8,128)S(1)}, u32[]{:S(2)}, u32[]{:S(2)}) collective-permute-start(f32[1,32,1408]{2,1,0:T(8,128)S(1)} %broadcast_select_fusion.27), channel_id=19, source_target_pairs={{0,15},{1,0},{2,1},{3,2},{4,3},{5,4},{6,5},{7,6},{8,7},{9,8},{10,9... | collective-permute-start | bytes 540680 | tf_op jit(solution)/vmap(transpose(jvp()))/dot_general | solution.py:20
  842.2 9.4 %collective-permute-start.6 = (f32[1,32,1408]{2,1,0:T(8,128)S(1)}, f32[1,32,1408]{2,1,0:T(8,128)S(1)}, u32[]{:S(2)}, u32[]{:S(2)}) collective-permute-start(f32[1,32,1408]{2,1,0:T(8,128)S(1)} %get-tuple-element.470), channel_id=22, source_target_pairs={{0,1},{1,2},{2,3},{3,4},{4,5},{5,6},{6,7},{7,8},{8,9},{9,10},{10,1... | collective-permute-start | bytes 540680 | tf_op jit(solution)/vmap(transpose(jvp()))/dot_general | solution.py:20
  851.7 12.0 %collective-permute-start.4 = (f32[1,32,1408]{2,1,0:T(8,128)S(1)}, f32[1,32,1408]{2,1,0:T(8,128)S(1)}, u32[]{:S(2)}, u32[]{:S(2)}) collective-permute-start(f32[1,32,1408]{2,1,0:T(8,128)S(1)} %broadcast_select_fusion.26), channel_id=20, source_target_pairs={{0,1},{1,2},{2,3},{3,4},{4,5},{5,6},{6,7},{7,8},{8,9},{9,10},{10,1... | collective-permute-start | bytes 540680 | tf_op jit(solution)/vmap(transpose(jvp()))/dot_general | solution.py:20
  851.8 12.0 %collective-permute-start.5 = (f32[1,32,1408]{2,1,0:T(8,128)S(1)}, f32[1,32,1408]{2,1,0:T(8,128)S(1)}, u32[]{:S(2)}, u32[]{:S(2)}) collective-permute-start(f32[1,32,1408]{2,1,0:T(8,128)S(1)} %broadcast_select_fusion.27), channel_id=19, source_target_pairs={{0,15},{1,0},{2,1},{3,2},{4,3},{5,4},{6,5},{7,6},{8,7},{9,8},{10,9... | collective-permute-start | bytes 540680 | tf_op jit(solution)/vmap(transpose(jvp()))/dot_general | solution.py:20
  863.8 9.4 %collective-permute-start.6 = (f32[1,32,1408]{2,1,0:T(8,128)S(1)}, f32[1,32,1408]{2,1,0:T(8,128)S(1)}, u32[]{:S(2)}, u32[]{:S(2)}) collective-permute-start(f32[1,32,1408]{2,1,0:T(8,128)S(1)} %get-tuple-element.470), channel_id=22, source_target_pairs={{0,1},{1,2},{2,3},{3,4},{4,5},{5,6},{6,7},{7,8},{8,9},{9,10},{10,1... | collective-permute-start | bytes 540680 | tf_op jit(solution)/vmap(transpose(jvp()))/dot_general | solution.py:20
  873.3 15.2 %collective-permute-start.27 = (f32[1,32,1408]{2,1,0:T(8,128)S(1)}, f32[1,32,1408]{2,1,0:T(8,128)S(1)}, u32[]{:S(2)}, u32[]{:S(2)}) collective-permute-start(f32[1,32,1408]{2,1,0:T(8,128)S(1)} %get-tuple-element.43), channel_id=35, source_target_pairs={{0,1},{1,2},{2,3},{3,4},{4,5},{5,6},{6,7},{7,8},{8,9},{9,10},{10,1... | collective-permute-start | bytes 540680 | tf_op jit(solution)/vmap(transpose(jvp()))/dot_general | solution.py:21
  (77 other events, 1386.0 us)
Sparse Core Ops, SparseCore 0:
  9.6 39.3 all-gather.36
  50.7 34.1 all-gather.28
  86.5 34.0 all-gather.30
  122.1 34.1 all-gather.32
  157.7 34.0 all-gather.38
  193.4 34.1 all-gather.34
where the time goes:
time: 915 us; the launch traced here: 904 us
  matrix products  445 us (49%)
  starting transfers between devices  145 us (16%)
  waiting for transfers between devices  100 us (11%)
  local copies, waits for them, and re-layouts  83.6 us (9%)
  other arithmetic  64.1 us (7%)
  loops' own time  49.6 us (5%)
  between operations  15.1 us (2%)
    dot_general x20, matrix products, layer(): gate = jnp.dot(a, w['w_gate'], preferred_element_type=jnp.float32)  173 us
    dot_general x20, matrix products, layer(): up = jnp.dot(a, w['w_up'], preferred_element_type=jnp.float32)  162 us
    dot_general x19, matrix products, matmul(): jnp.dot(a, w, preferred_element_type=jnp.float32).astype(jnp.bfloat16)  110 us
    squeeze x6, waiting for transfers between devices, stack(): h = layer(h, {name: w[number] for name, w in weights.items()})  94.6 us
    unnamed x73, local copies, waits for them, and re-layouts  63.8 us
    dot_general x34, starting transfers between devices, layer(): up = jnp.dot(a, w['w_up'], preferred_element_type=jnp.float32)  48.3 us
    dot_general x34, starting transfers between devices, layer(): gate = jnp.dot(a, w['w_gate'], preferred_element_type=jnp.float32)  48.3 us
    dot_general x34, starting transfers between devices, matmul(): jnp.dot(a, w, preferred_element_type=jnp.float32).astype(jnp.bfloat16)  48.3 us
  transfers between devices with their start and end apart: 108, of which 8 were waited for; matrix products, arithmetic and copies ran while one was open for 57% of the time, Pallas kernels for 0%

commit v1 on v0

v1 whole, which is shorter than its diff:
```python
import functools

import jax
import jax.numpy as jnp
from jax import lax
from jax.experimental import pallas as pl
from jax.experimental.pallas import tpu as pltpu
from jax.sharding import PartitionSpec as P

BF16, F32 = jnp.bfloat16, jnp.float32
LANES = 128
TILE = 512
WIDTHS = (4, 4, 3)
EPS = 1e-6


def dot(a, b):
    return jnp.dot(a, b, preferred_element_type=F32)


def dot_nt(a, b):
    return lax.dot_general(a, b, (((1,), (1,)), ((), ())), preferred_element_type=F32)


def dot_tn(a, b):
    return lax.dot_general(a, b, (((0,), (0,)), ((), ())), preferred_element_type=F32)


def blocks(ff):
    start, out = 0, []
    widths = WIDTHS if sum(WIDTHS) * LANES == ff else (1,) * (ff // LANES)
    for w in widths:
        out.append((start, w * LANES))
        start += w * LANES
    return out


def norm(h):
    wide = h.astype(F32)
    scale = lax.rsqrt(jnp.mean(wide * wide, -1, keepdims=True) + EPS)
    return wide, scale, (wide * scale).astype(BF16)


def halves(gu, width):
    n = width // LANES
    gate = jnp.concatenate([gu[:, 2 * i * LANES : (2 * i + 1) * LANES] for i in range(n)], 1)
    up = jnp.concatenate([gu[:, (2 * i + 1) * LANES : (2 * i + 2) * LANES] for i in range(n)], 1)
    return gate, up


def woven(gate, up):
    n = gate.shape[1] // LANES
    parts = []
    for i in range(n):
        parts += [gate[:, i * LANES : (i + 1) * LANES], up[:, i * LANES : (i + 1) * LANES]]
    return jnp.concatenate(parts, 1)


def forward_kernel(x_ref, wgu_ref, wd_ref, h_ref, hid_ref):
    x, _, a = norm(x_ref[...])
    for start, width in blocks(hid_ref.shape[1]):
        gate, up = halves(dot(a, wgu_ref[:, 2 * start : 2 * (start + width)]), width)
        hid_ref[:, start : start + width] = (gate * jax.nn.sigmoid(gate) * up).astype(BF16)
    out = dot(hid_ref[...], wd_ref[...]).astype(BF16)
    h_ref[...] = (x + out.astype(F32)).astype(BF16)


def backward_kernel(h_ref, dy_ref, wgu_ref, wd_ref, dh_ref, dwgu_ref, dwd_ref, hid_ref, dgu_ref, acc_gu, acc_d):
    t = pl.program_id(0)

    @pl.when(t == 0)
    def _():
        acc_gu[...] = jnp.zeros_like(acc_gu)
        acc_d[...] = jnp.zeros_like(acc_d)

    wide, scale, a = norm(h_ref[...])
    dy = dy_ref[...]
    for start, width in blocks(hid_ref.shape[1]):
        gate, up = halves(dot(a, wgu_ref[:, 2 * start : 2 * (start + width)]), width)
        dhid = dot_nt(dy, wd_ref[start : start + width, :]).astype(BF16).astype(F32)
        s = jax.nn.sigmoid(gate)
        act = gate * s
        hid_ref[:, start : start + width] = (act * up).astype(BF16)
        dgate = dhid * up * (s + act * (1.0 - s))
        dup = dhid * act
        dgu_ref[:, 2 * start : 2 * (start + width)] = woven(dgate.astype(BF16), dup.astype(BF16))
    acc_d[...] += dot_tn(hid_ref[...], dy)
    acc_gu[...] += dot_tn(a, dgu_ref[...])
    da = dot_nt(dgu_ref[...], wgu_ref[...]).astype(BF16).astype(F32)
    inner = jnp.mean(da * wide, -1, keepdims=True) * (scale * scale * scale)
    dn = (da * scale - wide * inner).astype(BF16)
    dh_ref[...] = (dy.astype(F32) + dn.astype(F32)).astype(BF16)

    @pl.when(t == pl.num_programs(0) - 1)
    def _():
        dwgu_ref[...] = acc_gu[...].astype(BF16)
        dwd_ref[...] = acc_d[...].astype(BF16)


def params():
    return pltpu.CompilerParams(dimension_semantics=("arbitrary",), vmem_limit_bytes=60 * 2**20)


def once(shape):
    return pl.BlockSpec(shape, lambda t: (0, 0))


def rows(d):
    return pl.BlockSpec((TILE, d), lambda t: (t, 0))


def forward(x, wgu, wd):
    tokens, d = x.shape
    ff = wd.shape[0]
    return pl.pallas_call(
        forward_kernel,
        grid=(tokens // TILE,),
        in_specs=[rows(d), once(wgu.shape), once(wd.shape)],
        out_specs=rows(d),
        out_shape=jax.ShapeDtypeStruct(x.shape, BF16),
        scratch_shapes=[pltpu.VMEM((TILE, ff), BF16)],
        compiler_params=params(),
        cost_estimate=pl.CostEstimate(flops=6 * tokens * d * ff, bytes_accessed=4 * tokens * d, transcendentals=0),
        name="forward",
    )(x, wgu, wd)


def backward(h, dy, wgu, wd):
    tokens, d = h.shape
    ff = wd.shape[0]
    return pl.pallas_call(
        backward_kernel,
        grid=(tokens // TILE,),
        in_specs=[rows(d), rows(d), once(wgu.shape), once(wd.shape)],
        out_specs=[rows(d), once(wgu.shape), once(wd.shape)],
        out_shape=[jax.ShapeDtypeStruct(s, BF16) for s in (h.shape, wgu.shape, wd.shape)],
        scratch_shapes=[
            pltpu.VMEM((TILE, ff), BF16),
            pltpu.VMEM((TILE, 2 * ff), BF16),
            pltpu.VMEM(wgu.shape, F32),
            pltpu.VMEM(wd.shape, F32),
        ],
        compiler_params=params(),
        cost_estimate=pl.CostEstimate(flops=16 * tokens * d * ff, bytes_accessed=6 * tokens * d, transcendentals=0),
        name="backward",
    )(h, dy, wgu, wd)


def weave(gate, up):
    shape = gate.shape
    pair = jnp.stack([t.reshape(*shape[:-1], -1, LANES) for t in (gate, up)], -2)
    return pair.reshape(*shape[:-1], -1)


def unweave(both):
    shape = both.shape
    pair = both.reshape(*shape[:-1], -1, 2, LANES)
    return tuple(pair[..., i, :].reshape(*shape[:-1], -1) for i in range(2))


def solution(mesh):
    def step(x, dy, w_gate, w_up, w_down):
        layers = w_gate.shape[0]
        wgu = weave(w_gate, w_up)
        gathered = [
            tuple(lax.all_gather(w[i], "dp", axis=0, tiled=True) for w in (wgu, w_down)) for i in range(layers)
        ]
        h = [x[0]]
        for i in range(layers - 1):
            h.append(forward(h[-1], *gathered[i]))
        by = dy[0]
        grads = [None] * layers
        for i in reversed(range(layers)):
            by, dwgu, dwd = backward(h[i], by, *gathered[i])
            grads[i] = tuple(lax.psum_scatter(t, "dp", scatter_dimension=0, tiled=True) for t in (dwgu, dwd))
        dgate, dup = unweave(jnp.stack([g[0] for g in grads]))
        return by[None], dgate, dup, jnp.stack([g[1] for g in grads])

    tokens, weight = P(("rep", "dp"), None, None), P(None, "dp", None)
    out = P("rep", "dp", None)
    return jax.shard_map(
        step, mesh=mesh, in_specs=(tokens, tokens, weight, weight, weight), out_specs=(tokens, out, out, out), check_vma=False
    )
```

time: 915 us -> 522 us (0.57); the launches traced: 904 us -> 522 us
  matrix products: 445 us -> 0 us
  waiting for transfers between devices: 100 us -> 350 us
  Pallas kernels: 0 us -> 146 us
  starting transfers between devices: 145 us -> 0.5 us
  local copies, waits for them, and re-layouts: 83.6 us -> 9.36 us
  other arithmetic: 64.1 us -> 1.62 us
  loops' own time: 49.6 us -> 0 us
    dot_general x59 -> x0, matrix products: 445 us -> none  [the longest x20 173 us: layer(): gate = jnp.dot(a, w['w_gate'], preferred_element_type=jnp.float32)]
    reduce_scatter x0 -> x4, waiting for transfers between devices: none -> 224 us  [step(): lax.psum_scatter(t, 'dp', scatter_dimension=0, tiled=True)]
    pallas_call x0 -> x3, Pallas kernels: none -> 146 us  [the longest x2 122 us: backward(): pl.pallas_call(backward_kernel, grid=(tokens // TILE,), in_specs=[rows(d)...]
    dot_general x102 -> x0, starting transfers between devices: 145 us -> none  [the longest x34 48.3 us: layer(): up = jnp.dot(a, w['w_up'], preferred_element_type=jnp.float32)]
    all_gather x0 -> x4, waiting for transfers between devices: none -> 123 us  [step(): lax.all_gather(w[i], 'dp', axis=0, tiled=True)]
    squeeze x6 -> x0, waiting for transfers between devices: 94.6 us -> none  [stack(): h = layer(h, {name: w[number] for name, w in weights.items()})]
    unnamed x73 -> x2, local copies, waits for them, and re-layouts: 63.8 us -> 0.06 us
    another operation x6 -> x0, loops' own time: 49.6 us -> none  [the longest x2 16.7 us: layer(): up = jnp.dot(a, w['w_up'], preferred_element_type=jnp.float32)]
  transfers between devices with their start and end apart: 108 -> 8, of which waited for: 8 -> 8; matrix products, arithmetic and copies ran while one was open for 57% -> 1% of each run, Pallas kernels for 0% -> 5%
where the time goes in v1:
time: 522 us
  waiting for transfers between devices  350 us (67%)
  Pallas kernels  146 us (28%)
  between operations  14.2 us (3%)
  local copies, waits for them, and re-layouts  9.36 us (2%)
    reduce_scatter x4, waiting for transfers between devices, step(): lax.psum_scatter(t, 'dp', scatter_dimension=0, tiled=True)  224 us
    all_gather x4, waiting for transfers between devices, step(): lax.all_gather(w[i], 'dp', axis=0, tiled=True)  123 us
    pallas_call x2, Pallas kernels, backward(): pl.pallas_call(backward_kernel, grid=(tokens // TILE,), in_specs=[rows(d)...  122 us
    pallas_call x1, Pallas kernels, forward(): pl.pallas_call(forward_kernel, grid=(tokens // TILE,), in_specs=[rows(d),...  23.8 us
  transfers between devices with their start and end apart: 8, of which 8 were waited for; matrix products, arithmetic and copies ran while one was open for 1% of the time, Pallas kernels for 5%

profile of v1, /device:TPU:22, one launch (start us, length us, event | category | flops | bytes accessed | tf_op | source)
XLA Modules:
  0.0 521.5 jit_solution(909847507856634932)
XLA Ops:
  7.2 0.1 all-gather.11.cloned.1.call-start
  7.2 1.6 fusion.2
  8.9 0.1 all-gather.11.cloned.1.call-update
  8.9 0.1 all-gather.7.cloned.1.call-start
  9.0 1.1 stack_reshape.6
  10.1 1.1 stack_reshape.7
  11.2 0.2 copy.11
  11.4 0.7 squeeze.19
  12.2 0.1 all-gather.7.cloned.1.call-update
  12.2 0.1 all-gather.13.cloned.1.call-start
  12.3 0.7 all-gather.13.cloned.1.call-update
  13.0 0.1 all-gather.9.cloned.1.call-start
  13.1 0.2 copy.12
  13.3 0.7 squeeze.22
  14.1 0.1 all-gather.9.cloned.1.call-update
  14.1 0.1 reduce-scatter.9.cloned.1.call-start
  14.2 35.4 %all-gather.11.cloned.1.call-done = bf16[1,1408,512]{2,1,0:T(8,128)(2,1)} async-done(((bf16[1,88,512]{2,1,0:T(8,128)(2,1)}), bf16[1,1408,512]{2,1,0:T(8,128)(2,1)}) %all-gather.11.cloned.1.call-update) | async-done | bytes 1441808 | tf_op jit(solution)/shard_map/all_gather | solution.py:166
  49.6 37.5 %all-gather.7.cloned.1.call-done.wgu_ref = bf16[512,2816]{1,0:T(8,128)(2,1)} async-done(((bf16[32,2816]{1,0:T(8,128)(2,1)}), bf16[512,2816]{1,0:T(8,128)(2,1)}) %all-gather.7.cloned.1.call-update) | async-done | bytes 2883600 | tf_op jit(solution)/shard_map/all_gather | solution.py:166
  87.2 23.8 %forward.1.h_ref = bf16[4096,512]{1,0:T(8,128)(2,1)} custom-call(bf16[4096,512]{1,0:T(8,128)(2,1)} %bitcast.14, bf16[512,2816]{1,0:T(8,128)(2,1)} %all-gather.7.cloned.1.call-done.wgu_ref, bf16[1408,512]{1,0:T(8,128)(2,1)} %bitcast.16), custom_call_target="tpu_custom_call" | custom-call | flops 17716740096 | bytes 8388608 | tf_op jit(solution)/shard_map/forward/pallas_call | solution.py:115
  111.0 12.8 %all-gather.13.cloned.1.call-done = bf16[1,1408,512]{2,1,0:T(8,128)(2,1)} async-done(((bf16[1,88,512]{2,1,0:T(8,128)(2,1)}), bf16[1,1408,512]{2,1,0:T(8,128)(2,1)}) %all-gather.13.cloned.1.call-update) | async-done | bytes 1441808 | tf_op jit(solution)/shard_map/all_gather | solution.py:166
  123.8 37.4 %all-gather.9.cloned.1.call-done.wgu_ref = bf16[512,2816]{1,0:T(8,128)(2,1)} async-done(((bf16[32,2816]{1,0:T(8,128)(2,1)}), bf16[512,2816]{1,0:T(8,128)(2,1)}) %all-gather.9.cloned.1.call-update) | async-done | bytes 2883600 | tf_op jit(solution)/shard_map/all_gather | solution.py:166
  161.2 61.0 %backward.2 = (bf16[4096,512]{1,0:T(8,128)(2,1)}, bf16[512,2816]{1,0:T(8,128)(2,1)}, bf16[1408,512]{1,0:T(8,128)(2,1)}) custom-call(bf16[4096,512]{1,0:T(8,128)(2,1)} %forward.1.h_ref, bf16[4096,512]{1,0:T(8,128)(2,1)} %bitcast.13, bf16[512,2816]{1,0:T(8,128)(2,1)} %all-gather.9.cloned.1.call-done.wgu_ref, bf16[1408,512]{1,0:T(8,128)(2,1)} %bitcast.18), custom_call_target="tpu_custom_call" | custom-call | flops 47244640256 | bytes 12582912 | tf_op jit(solution)/shard_map/backward/pallas_call | solution.py:131
  222.1 61.2 %backward.3 = (bf16[4096,512]{1,0:T(8,128)(2,1)}, bf16[512,2816]{1,0:T(8,128)(2,1)}, bf16[1408,512]{1,0:T(8,128)(2,1)}) custom-call(bf16[4096,512]{1,0:T(8,128)(2,1)} %bitcast.15, bf16[4096,512]{1,0:T(8,128)(2,1)} %get-tuple-element.10.dy_ref, bf16[512,2816]{1,0:T(8,128)(2,1)} %all-gather.7.cloned.1.call-done.wgu_ref, bf16[1408,512]{1,0:T(8,128)(2,1)} %bitcast.17), custom_call_target="tpu_custom_call" | custom-call | flops 47244640256 | bytes 12582912 | tf_op jit(solution)/shard_map/backward/pallas_call | solution.py:131
  283.3 0.1 reduce-scatter.9.cloned.1.call-update
  283.4 0.1 reduce-scatter.11.cloned.1.call-start
  283.5 0.6 reduce-scatter.11.cloned.1.call-update
  284.0 0.1 reduce-scatter.5.cloned.1.call-start
  284.1 0.7 reduce-scatter.5.cloned.1.call-update
  284.8 0.1 reduce-scatter.7.cloned.1.call-start
  284.9 0.7 reduce-scatter.7.cloned.1.call-update
  285.6 52.1 %reduce-scatter.9.cloned.1.call-done = bf16[88,512]{1,0:T(8,128)(2,1)} async-done(((bf16[1408,512]{1,0:T(8,128)(2,1)}), bf16[88,512]{1,0:T(8,128)(2,1)}) %reduce-scatter.9.cloned.1.call-update) | async-done | bytes 90128 | tf_op jit(solution)/shard_map/reduce_scatter | solution.py:175
  337.7 56.4 %reduce-scatter.11.cloned.1.call-done = bf16[88,512]{1,0:T(8,128)(2,1)} async-done(((bf16[1408,512]{1,0:T(8,128)(2,1)}), bf16[88,512]{1,0:T(8,128)(2,1)}) %reduce-scatter.11.cloned.1.call-update) | async-done | bytes 90128 | tf_op jit(solution)/shard_map/reduce_scatter | solution.py:175
  394.2 1.6 pad_maximum_fusion
  395.8 57.4 %reduce-scatter.5.cloned.1.call-done = bf16[32,2816]{1,0:T(8,128)(2,1)} async-done(((bf16[512,2816]{1,0:T(8,128)(2,1)}), bf16[32,2816]{1,0:T(8,128)(2,1)}) %reduce-scatter.5.cloned.1.call-update) | async-done | bytes 180240 | tf_op jit(solution)/shard_map/reduce_scatter | solution.py:175
  453.2 1.0 stack.22
  454.2 57.8 %reduce-scatter.7.cloned.1.call-done = bf16[32,2816]{1,0:T(8,128)(2,1)} async-done(((bf16[512,2816]{1,0:T(8,128)(2,1)}), bf16[32,2816]{1,0:T(8,128)(2,1)}) %reduce-scatter.7.cloned.1.call-update) | async-done | bytes 180240 | tf_op jit(solution)/shard_map/reduce_scatter | solution.py:175
  512.0 1.0 stack.23
  512.9 0.1 copy_dynamic-update-slice_fusion
  513.1 0.8 reshape_squeeze.7
  513.9 0.8 reshape_squeeze.6
  (5 shorter events, 0.2 us)
Async XLA Ops:
  7.2 42.5 %all-gather.11.cloned.1.call-start = ((), (), s32[]{:S(2)}) async-start(), calls=%async_computation.10 | async-start | bytes 1531904 | tf_op jit(solution)/shard_map/all_gather | solution.py:166
  8.9 78.3 %all-gather.7.cloned.1.call-start = ((), (), s32[]{:S(2)}) async-start(), calls=%async_computation.4 | async-start | bytes 3063808 | tf_op jit(solution)/shard_map/all_gather | solution.py:166
  12.2 111.5 %all-gather.13.cloned.1.call-start = ((), (), s32[]{:S(2)}) async-start(), calls=%async_computation.11 | async-start | bytes 1531904 | tf_op jit(solution)/shard_map/all_gather | solution.py:166
  13.0 148.1 %all-gather.9.cloned.1.call-start = ((), (), s32[]{:S(2)}) async-start(), calls=%async_computation.5 | async-start | bytes 3063808 | tf_op jit(solution)/shard_map/all_gather | solution.py:166
  14.1 323.6 %reduce-scatter.9.cloned.1.call-start = ((), (), s32[]{:S(2)}) async-start(), calls=%async_computation.8 | async-start | bytes 1531904 | tf_op jit(solution)/shard_map/reduce_scatter | solution.py:175
  283.4 110.8 %reduce-scatter.11.cloned.1.call-start = ((), (), s32[]{:S(2)}) async-start(), calls=%async_computation.9 | async-start | bytes 1531904 | tf_op jit(solution)/shard_map/reduce_scatter | solution.py:175
  284.0 169.2 %reduce-scatter.5.cloned.1.call-start = ((), (), s32[]{:S(2)}) async-start(), calls=%async_computation.6 | async-start | bytes 3063808 | tf_op jit(solution)/shard_map/reduce_scatter | solution.py:175
  284.8 227.1 %reduce-scatter.7.cloned.1.call-start = ((), (), s32[]{:S(2)}) async-start(), calls=%async_computation.7 | async-start | bytes 3063808 | tf_op jit(solution)/shard_map/reduce_scatter | solution.py:175
Sparse Core Ops, SparseCore 0:
  10.2 39.3 all-gather.10
  51.8 35.2 all-gather.6
  89.4 34.3 all-gather.12
  125.8 35.3 all-gather.8
  283.5 54.1 reduce-scatter.8
  339.9 54.1 reduce-scatter.10
  396.5 56.6 reduce-scatter.4
  455.5 56.4 reduce-scatter.6
